TPU v7x, 32 devices: a whole 2x2x4 slice. The times are simulated.
32 devices in a mesh: group: 2 (over y), row: 4 (over z), col: 4 (over x, core).
Axes of the slice: x: 2, y: 2, z: 4, core: 2. Of those that a mesh axis runs over, the one named last changes fastest.
Arguments:
- compressed_absorbed_queries: bfloat16 [16, 128, 512], P(('group', 'row')), parts along dimension 0, may hold values from -6 to 6
- query_rope: bfloat16 [16, 64, 128], P(('group', 'row')), parts along dimension 0, may hold values from -6 to 6
- compressed_stored_keys: bfloat16 [16, 1024, 512], P(('group', 'row'), 'col'), parts along dimension 0, may hold values from -32 to 32
- cache_rope: bfloat16 [16, 64, 1024], P(('group', 'row'), None, 'col'), parts along dimension 0, may hold values from -32 to 32
- seq_lengths: int32 [16], P(('group', 'row')), parts along dimension 0, may hold values from 2 to 1024, as said below
- ffn_rows: bfloat16 [64, 7168], P(('group', 'row'), 'col'), parts along dimension 0, may hold values from -6 to 6
- norm_gain: bfloat16 [7168], P('col'), may hold values from 0.099609375 to 1.8984375
- w_gate: bfloat16 [7168, 18432], P('col', 'row'), may hold values from -0.0625 to 0.0625
- w_up: bfloat16 [7168, 18432], P('col', 'row'), may hold values from -0.0625 to 0.0625
- w_down: bfloat16 [18432, 7168], P('row', 'col'), may hold values from -0.046875 to 0.046875
Outputs:
- context: bfloat16 [16, 128, 512], P(('group', 'row'), 'col'), parts along dimension 0
- ffn_out: bfloat16 [64, 7168], P(('group', 'row'), 'col'), parts along dimension 0
There are 2 independent parts, one for each index of `group`. A program takes and returns all parts, laid end to end along the dimension named above; an argument that names none is the same for every part. Nothing has to cross between parts.
Inputs may be any that keep to these rules, and one draw needn't show every extreme that they name: `seq_lengths`: each sequence has 2 to 1024 filled slots, the first ones of its cache, and some sequence has exactly 1024.
All inputs are finite; a program needn't handle non-finite values.
Results may differ from a plain program's by a relative error of at most 0.017.
Values may be sent and summed in bfloat16 or wider, within the bound.
A program may use at most 128 MiB of HBM per device.

v0:
```python
import jax
import jax.numpy as jnp
from jax import lax
from jax.sharding import PartitionSpec as P

NOPE = 128


NEGATIVE_PADDING = -1e30


def joined(x, axis, combine):
    everything = jax.tree.map(
        lambda part, kind: lax.all_gather(part.astype(kind), axis),
        x,
        (jnp.bfloat16, jnp.bfloat16, jnp.bfloat16),
    )

    def take(k):
        return jax.tree.map(lambda part, own: part[k].astype(own.dtype), everything, x)

    return lax.fori_loop(
        1, lax.axis_size(axis), lambda k, so_far: combine(so_far, take(k)), take(0)
    )


def local_partials(
    compressed_absorbed_queries,
    query_rope,
    compressed_stored_keys,
    cache_rope,
    seq_lengths,
    first_pos,
):
    similarity_logits = jnp.einsum(
        "zxm,zum->zxu",
        compressed_absorbed_queries,
        compressed_stored_keys,
        preferred_element_type=jnp.float32,
    )
    similarity_logits = similarity_logits + jnp.einsum(
        "srh,srl->shl", query_rope, cache_rope, preferred_element_type=jnp.float32
    )
    similarity_logits = similarity_logits * (NOPE + query_rope.shape[1]) ** (-0.5)
    position = first_pos + jnp.arange(compressed_stored_keys.shape[1], dtype=jnp.int32)
    visible = position[None, None, :] < seq_lengths[:, None, None]
    similarity_logits = jnp.where(visible, similarity_logits, NEGATIVE_PADDING)
    top_score = jnp.max(similarity_logits, axis=2)
    weights = jnp.where(visible, jnp.exp(similarity_logits - top_score[:, :, None]), 0.0)
    denominator = jnp.sum(weights, axis=2)
    weighted = jnp.einsum(
        "jac,jcw->jaw",
        weights.astype(jnp.bfloat16),
        compressed_stored_keys,
        preferred_element_type=jnp.float32,
    )
    return (top_score, denominator, weighted)


def join_partials(earlier, later):
    top_score = jnp.maximum(earlier[0], later[0])
    left_factor = jnp.exp(earlier[0] - top_score)
    right_factor = jnp.exp(later[0] - top_score)
    denominator = earlier[1] * left_factor + later[1] * right_factor
    weighted = earlier[2] * left_factor[:, :, None] + later[2] * right_factor[:, :, None]
    return (top_score, denominator, weighted)


def on_device(
    compressed_absorbed_queries,
    query_rope,
    compressed_stored_keys,
    cache_rope,
    seq_lengths,
    ffn_rows,
    norm_gain,
    w_gate,
    w_up,
    w_down,
):
    column_position = lax.axis_index("col")
    first_pos = column_position * compressed_stored_keys.shape[1]
    top_score, denominator, weighted = local_partials(
        compressed_absorbed_queries,
        query_rope,
        compressed_stored_keys,
        cache_rope,
        seq_lengths,
        first_pos,
    )
    head_share = compressed_absorbed_queries.shape[1] // lax.axis_size("col")
    merged = joined((top_score, denominator, weighted), "col", join_partials)
    own_total = lax.dynamic_slice_in_dim(merged[1], column_position * head_share, head_share, 1)
    own_weighted = lax.dynamic_slice_in_dim(merged[2], column_position * head_share, head_share, 1)
    context = (own_weighted / own_total[:, :, None]).astype(jnp.bfloat16)
    rows_wide = ffn_rows.astype(jnp.float32)
    square_sums = lax.psum(jnp.sum(rows_wide * rows_wide, axis=1), "col")
    full_width = ffn_rows.shape[1] * lax.axis_size("col")
    reciprocal_norm = lax.rsqrt(square_sums / full_width + 1e-06)
    normed = (rows_wide * reciprocal_norm[:, None] * norm_gain.astype(jnp.float32)[None, :]).astype(
        jnp.bfloat16
    )
    shard_rows = lax.all_gather(normed, "row", axis=0, tiled=True)
    gate_part = jnp.dot(shard_rows, w_gate, preferred_element_type=jnp.float32)
    up_part = jnp.dot(shard_rows, w_up, preferred_element_type=jnp.float32)
    projected = jnp.concatenate([gate_part, up_part], axis=1)
    units = w_gate.shape[1]
    share_sums = lax.psum_scatter(
        projected.astype(jnp.bfloat16), "col", scatter_dimension=0, tiled=True
    ).astype(jnp.float32)
    hidden_share = (jax.nn.silu(share_sums[:, :units]) * share_sums[:, units:]).astype(jnp.bfloat16)
    hidden = lax.all_gather(hidden_share, "col", axis=0, tiled=True)
    reduced_total = lax.psum_scatter(
        jnp.dot(hidden, w_down, preferred_element_type=jnp.float32),
        "row",
        scatter_dimension=0,
        tiled=True,
    )
    ffn_out = (rows_wide + reduced_total).astype(jnp.bfloat16)
    return (context, ffn_out)


def solution(mesh):
    return jax.shard_map(
        on_device,
        mesh=mesh,
        in_specs=(
            P(("group", "row"), None, None),
            P(("group", "row"), None, None),
            P(("group", "row"), "col", None),
            P(("group", "row"), None, "col"),
            P(("group", "row")),
            P(("group", "row"), "col"),
            P("col"),
            P("col", "row"),
            P("col", "row"),
            P("row", "col"),
        ),
        out_specs=(P(("group", "row"), "col", None), P(("group", "row"), "col")),
        check_vma=False,
    )
```

profile of v0, /device:TPU:0, one launch (start us, length us, event | category | flops | bytes accessed | tf_op | source)
XLA Modules:
  0.0 115.1 jit_solution(4013423057301016343)
XLA Ops:
  7.2 0.0 copy-start
  7.2 0.0 reduce-scatter.3.cloned.1.call-start
  7.2 0.9 fusion.14
  8.2 0.7 convert_element_type.125
  8.8 8.3 %psum.7 = f32[8]{0:T(128)S(1)} all-reduce(f32[8]{0:T(128)S(1)} %fusion.14), channel_id=1, replica_groups=mesh['group'=2,'row'=4,'col'=4] {'col'}, use_global_device_ids=true, to_apply=%region_5.6 | all-reduce | flops 8 | bytes 64 | tf_op jit(solution)/shard_map/psum | solution.py:97
  17.2 1.0 fusion.16
  18.2 13.7 %all_gather.24 = bf16[32,1792]{1,0:T(8,128)(2,1)S(1)} all-gather(bf16[8,1792]{1,0:T(8,128)(2,1)S(1)} %fusion.16), channel_id=1, replica_groups=mesh['group'=2,'row'=4,'col'=4] {'row'}, dimensions={0}, use_global_device_ids=true | all-gather | bytes 143360 | tf_op jit(solution)/shard_map/all_gather | solution.py:103
  31.9 8.6 %convolution_convert_fusion = bf16[32,4608]{1,0:T(8,128)(2,1)S(1)} fusion(bf16[32,1792]{1,0:T(8,128)(2,1)S(1)} %all_gather.24, bf16[1792,4608]{1,0:T(8,128)(2,1)} %param.20), kind=kOutput, calls=%fused_computation.12 | convolution fusion | flops 528629760 | bytes 16924672 | tf_op jit(solution)/shard_map/dot_general | solution.py:105
  40.5 0.0 copy-done.1
  40.5 0.0 copy-start.4
  40.5 0.0 copy-start.5
  40.6 0.0 copy-start.2
  40.6 2.9 %convolution_convert_fusion.1 = bf16[32,4608]{1,0:T(8,128)(2,1)S(1)} fusion(bf16[32,1792]{1,0:T(8,128)(2,1)S(1)} %all_gather.24, bf16[1792,4608]{1,0:T(8,128)(2,1)S(1)} %copy-done.1), kind=kOutput, calls=%fused_computation.13 | convolution fusion | flops 528629760 | bytes 16924672 | tf_op jit(solution)/shard_map/dot_general | solution.py:104
  43.5 0.9 pad_maximum_fusion
  44.4 0.0 reduce-scatter.3.cloned.1.call-update
  44.4 0.0 all-gather.7.cloned.1.call-start
  44.4 0.0 copy-done.6
  44.5 0.1 broadcast_compare_fusion
  44.5 0.0 copy-done.4
  44.5 0.0 copy-done.5
  44.5 0.2 fusion.23
  44.8 0.0 copy-done
  44.8 0.0 copy-done.2
  44.8 0.4 fusion.22
  45.2 1.0 convolution_convert_fusion.2
  46.2 0.0 all-gather.7.cloned.1.call-update
  46.2 0.0 reduce-scatter.5.cloned.1.call-start
  46.2 0.2 fusion.8
  46.4 5.1 %all-gather.4 = bf16[4,2,128]{2,1,0:T(2,128)(2,1)S(1)} all-gather(bf16[1,2,128]{2,1,0:T(2,128)(2,1)S(1)} %bitcast.49), channel_id=3, replica_groups=mesh['group'=2,'row'=4,'col'=4] {'col'}, dimensions={0}, use_global_device_ids=true | all-gather | bytes 2560 | tf_op jit(solution)/shard_map/all_gather | solution.py:14
  51.5 5.0 %all-gather.3 = bf16[4,2,128]{2,1,0:T(2,128)(2,1)S(1)} all-gather(bf16[1,2,128]{2,1,0:T(2,128)(2,1)S(1)} %convert_bitcast_fusion.1), channel_id=2, replica_groups=mesh['group'=2,'row'=4,'col'=4] {'col'}, dimensions={0}, use_global_device_ids=true | all-gather | bytes 2560 | tf_op jit(solution)/shard_map/all_gather | solution.py:14
  56.6 10.2 %reduce-scatter.3.cloned.1.call-done = bf16[8,9216]{1,0:T(8,128)(2,1)} async-done(((bf16[32,9216]{1,0:T(8,128)(2,1)}), bf16[8,9216]{1,0:T(8,128)(2,1)}) %reduce-scatter.3.cloned.1.call-update) | async-done | bytes 147472 | tf_op jit(solution)/shard_map/reduce_scatter | solution.py:108
  66.8 0.9 convert_element_type.127
  67.7 0.1 fusion.9
  67.8 0.0 copy-start.3
  67.8 5.9 %all_gather.25 = bf16[32,4608]{1,0:T(8,128)(2,1)S(1)} all-gather(bf16[8,4608]{1,0:T(8,128)(2,1)S(1)} %fusion.9), channel_id=1, replica_groups=mesh['group'=2,'row'=4,'col'=4] {'col'}, dimensions={0}, use_global_device_ids=true | all-gather | bytes 368640 | tf_op jit(solution)/shard_map/all_gather | solution.py:112
  73.6 9.6 %fusion.24 = f32[32,1792]{1,0:T(8,128)} fusion(bf16[32,4608]{1,0:T(8,128)(2,1)S(1)} %all_gather.25, bf16[4608,1792]{1,0:T(8,128)(2,1)} %param.21), kind=kOutput, calls=%fused_computation.49 | convolution fusion | flops 528482304 | bytes 17039360 | tf_op jit(solution)/shard_map/dot_general | solution.py:114
  83.3 0.0 reduce-scatter.5.cloned.1.call-update
  83.3 1.8 %all-gather.7.cloned.1.call-done = bf16[8,128,512]{2,1,0:T(8,128)(2,1)} async-done(((bf16[2,128,512]{2,1,0:T(8,128)(2,1)}), bf16[8,128,512]{2,1,0:T(8,128)(2,1)}) %all-gather.7.cloned.1.call-update) | async-done | bytes 1048592 | tf_op jit(solution)/shard_map/all_gather | solution.py:14
  85.1 1.0 slice_convert_fusion
  86.1 3.5 %while.19 = (s32[]{:T(128)}, f32[2,128]{1,0:T(2,128)S(1)}, f32[2,128]{1,0:T(2,128)S(1)}, f32[2,128,512]{2,1,0:T(8,128)S(1)}, bf16[4,2,128]{2,1,0:T(2,128)(2,1)S(...) while((s32[]{:T(128)}, f32[2,128]{1,0:T(2,128)S(1)}, ...), condition=%wide.region_3.4_spmd, body=%wide.region_2.3_spmd.sunk | while | flops 526341 | bytes 1320087 | solution.py:22
  86.1 1.1 fusion.39
  87.3 1.1 fusion.39
  88.5 1.1 fusion.39
  89.6 0.1 constant_dynamic-slice_fusion.2
  89.7 0.7 divide_convert_fusion
  90.4 16.8 %reduce-scatter.5.cloned.1.call-done = f32[8,1792]{1,0:T(8,128)} async-done(((f32[32,1792]{1,0:T(8,128)}), f32[8,1792]{1,0:T(8,128)}) %reduce-scatter.5.cloned.1.call-update) | async-done | bytes 57360 | tf_op jit(solution)/shard_map/reduce_scatter | solution.py:113
  107.2 0.0 copy-done.3
  107.2 1.4 %fusion.17 = bf16[8,1792]{1,0:T(8,128)(2,1)} fusion(f32[8,1792]{1,0:T(8,128)} %reduce-scatter.5.cloned.1.call-done, bf16[8,1792]{1,0:T(8,128)(2,1)S(1)} %copy-done.3), kind=kLoop, calls=%fused_computation.35 | loop fusion | flops 43008 | bytes 114688 | tf_op jit(solution)/shard_map/convert_element_type | solution.py:119
  (10 shorter events, 0.1 us)
Async XLA Ops:
  7.2 37.6 %copy-start = (bf16[2,256,512]{2,1,0:T(8,128)(2,1)S(1)}, bf16[2,256,512]{2,1,0:T(8,128)(2,1)}, u32[]{:S(2)}) copy-start(bf16[2,256,512]{2,1,0:T(8,128)(2,1)} %param.14) | copy-start | bytes 1572868
  7.2 59.6 %reduce-scatter.3.cloned.1.call-start = ((), (), s32[]{:S(2)}) async-start(), calls=%async_computation.2 | async-start | bytes 737280 | tf_op jit(solution)/shard_map/reduce_scatter | solution.py:108
  17.2 23.3 %copy-start.1 = (bf16[1792,4608]{1,0:T(8,128)(2,1)S(1)}, bf16[1792,4608]{1,0:T(8,128)(2,1)}, u32[]{:S(2)}) copy-start(bf16[1792,4608]{1,0:T(8,128)(2,1)} %param.19) | copy-start | bytes 49545220
  40.5 3.9 %copy-start.6 = (s32[2]{0:T(128)S(1)}, s32[2]{0:T(128)}, u32[]{:S(2)}) copy-start(s32[2]{0:T(128)} %param.16) | copy-start | bytes 28
  40.5 4.0 %copy-start.4 = (bf16[2,64,256]{2,1,0:T(8,128)(2,1)S(1)}, bf16[2,64,256]{2,1,0:T(8,128)(2,1)}, u32[]{:S(2)}) copy-start(bf16[2,64,256]{2,1,0:T(8,128)(2,1)} %param.15) | copy-start | bytes 196612
  40.5 4.0 %copy-start.5 = (bf16[2,64,128]{2,1,0:T(8,128)(2,1)S(1)}, bf16[2,64,128]{2,1,0:T(8,128)(2,1)}, u32[]{:S(2)}) copy-start(bf16[2,64,128]{2,1,0:T(8,128)(2,1)} %param.13) | copy-start | bytes 98308
  40.6 4.2 %copy-start.2 = (bf16[2,128,512]{2,1,0:T(8,128)(2,1)S(1)}, bf16[2,128,512]{2,1,0:T(8,128)(2,1)}, u32[]{:S(2)}) copy-start(bf16[2,128,512]{2,1,0:T(8,128)(2,1)} %param.12) | copy-start | bytes 786436
  44.4 40.7 %all-gather.7.cloned.1.call-start = ((), (), s32[]{:S(2)}) async-start(), calls=%async_computation.4 | async-start | bytes 1310720 | tf_op jit(solution)/shard_map/all_gather | solution.py:14
  46.2 61.0 %reduce-scatter.5.cloned.1.call-start = ((), (), s32[]{:S(2)}) async-start(), calls=%async_computation.3 | async-start | bytes 286720 | tf_op jit(solution)/shard_map/reduce_scatter | solution.py:113
  67.8 39.4 %copy-start.3 = (bf16[8,1792]{1,0:T(8,128)(2,1)S(1)}, bf16[8,1792]{1,0:T(8,128)(2,1)}, u32[]{:S(2)}) copy-start(bf16[8,1792]{1,0:T(8,128)(2,1)} %param.17) | copy-start | bytes 86020
Sparse Core Ops, SparseCore 0:
  44.5 22.2 reduce-scatter.2
  68.3 16.6 all-gather.6
  87.3 19.8 reduce-scatter.4
where the time goes:
time: 116 us; the launch traced here: 115 us
  blocking collectives  38.1 us (33%)
  waiting for transfers between devices  28.8 us (25%)
  matrix products  22.7 us (20%)
  between operations  13.9 us (12%)
  other arithmetic  11.3 us (10%)
    reduce_scatter x1, waiting for transfers between devices, on_device(): lax.psum_scatter(jnp.dot(hidden, w_down, preferred_element_type=jnp.float...  16.8 us
    all_gather x1, blocking collectives, on_device(): shard_rows = lax.all_gather(normed, 'row', axis=0, tiled=True)  13.7 us
    reduce_scatter x1, waiting for transfers between devices, on_device(): lax.psum_scatter(projected.astype(jnp.bfloat16), 'col', scatter_dimension...  10.2 us
    all_gather x2, blocking collectives, joined(): lax.all_gather(part.astype(kind), axis)  10.1 us
    dot_general x1, matrix products, on_device(): jnp.dot(hidden, w_down, preferred_element_type=jnp.float32)  9.63 us
    dot_general x1, matrix products, on_device(): up_part = jnp.dot(shard_rows, w_up, preferred_element_type=jnp.float32)  8.62 us
    psum x1, blocking collectives, on_device(): square_sums = lax.psum(jnp.sum(rows_wide * rows_wide, axis=1), 'col')  8.34 us
    all_gather x1, blocking collectives, on_device(): hidden = lax.all_gather(hidden_share, 'col', axis=0, tiled=True)  5.87 us
  transfers between devices with their start and end apart: 3, of which 3 were waited for; matrix products, arithmetic and copies ran while one was open for 15% of the time, Pallas kernels for 0%

commit v1 on v0

v1 whole, which is shorter than its diff:
```python
import functools

import jax
import jax.numpy as jnp
from jax import lax
from jax.experimental import pallas as pl
from jax.experimental.pallas import tpu as pltpu
from jax.sharding import PartitionSpec as P

NOPE = 128
NEGATIVE_PADDING = -1e30
F32 = jnp.float32
BF16 = jnp.bfloat16


def kernel(
    nrow, ncol, chunks,
    q_hbm, qr_hbm, k_hbm, kr_hbm, lens, x_hbm, gain_hbm, wg_hbm, wu_hbm, wd_hbm,
    ctx_ref, out_ref,
    q, qr, k, kr, gain, xall, xg, wg, wu, wd,
    att, stat, att_in, stat_in, sq, sq_in,
    gu, gu_in, hid, acc, dn, dn_in,
    in_sem, w_sem, x_ss, x_rs, att_ss, att_rs, stat_ss, stat_rs, sq_ss, sq_rs,
    gu_ss, gu_rs, h_ss, h_rs, dn_ss, dn_rs,
):
    r = lax.axis_index("row")
    c = lax.axis_index("col")
    seqs, heads, latent = q_hbm.shape
    rope = qr_hbm.shape[1]
    slots = k_hbm.shape[1]
    own_rows, feats = x_hbm.shape
    units = wg_hbm.shape[1]
    nb = units // chunks
    tokens = own_rows * nrow
    tb = tokens // ncol
    hs = heads // ncol

    small = [
        pltpu.make_async_copy(x_hbm, xall.at[r], in_sem.at[0]),
        pltpu.make_async_copy(gain_hbm, gain, in_sem.at[1]),
        pltpu.make_async_copy(q_hbm, q, in_sem.at[2]),
        pltpu.make_async_copy(qr_hbm, qr, in_sem.at[3]),
        pltpu.make_async_copy(k_hbm, k, in_sem.at[4]),
        pltpu.make_async_copy(kr_hbm, kr, in_sem.at[5]),
    ]
    for copy in small:
        copy.start()

    def weight_copies(j):
        if chunks == 1:
            return (
                pltpu.make_async_copy(wg_hbm, wg.at[0], w_sem.at[0, 0]),
                pltpu.make_async_copy(wu_hbm, wu.at[0], w_sem.at[1, 0]),
                pltpu.make_async_copy(wd_hbm, wd.at[0], w_sem.at[2, 0]),
            )
        cut = pl.ds(pl.multiple_of(j * nb, 128), nb)
        return (
            pltpu.make_async_copy(wg_hbm.at[:, cut], wg.at[j], w_sem.at[0, j]),
            pltpu.make_async_copy(wu_hbm.at[:, cut], wu.at[j], w_sem.at[1, j]),
            pltpu.make_async_copy(wd_hbm.at[cut, :], wd.at[j], w_sem.at[2, j]),
        )

    for j in range(chunks):
        copies = weight_copies(j)
        copies[0].start()
        copies[1].start()
    for j in range(chunks):
        weight_copies(j)[2].start()

    barrier = pltpu.get_barrier_semaphore()
    for d in range(1, nrow):
        pl.semaphore_signal(barrier, inc=1, device_id={"row": lax.rem(r + d, nrow)},
                            device_id_type=pl.DeviceIdType.MESH)
    for d in range(1, ncol):
        pl.semaphore_signal(barrier, inc=1, device_id={"col": lax.rem(c + d, ncol)},
                            device_id_type=pl.DeviceIdType.MESH)
    pl.semaphore_wait(barrier, nrow + ncol - 2)

    def remote(src, dst, send, recv, axis, peer):
        return pltpu.make_async_remote_copy(
            src_ref=src, dst_ref=dst, send_sem=send, recv_sem=recv,
            device_id={axis: peer}, device_id_type=pl.DeviceIdType.MESH)

    def x_copy(d, source):
        return remote(xall.at[r], xall.at[source], x_ss.at[d - 1], x_rs.at[d - 1],
                      "row", lax.rem(r + d, nrow))

    small[0].wait()
    for d in range(1, nrow):
        x_copy(d, r).start()

    def att_copies(d):
        peer = lax.rem(c + d, ncol)
        return (
            remote(att.at[peer], att_in.at[d - 1], att_ss.at[d - 1], att_rs.at[d - 1], "col", peer),
            remote(stat.at[peer], stat_in.at[d - 1], stat_ss.at[d - 1], stat_rs.at[d - 1], "col", peer),
        )

    for copy in small[1:]:
        copy.wait()
    position = c * slots + lax.broadcasted_iota(jnp.int32, (1, slots), 1)
    lane = lax.broadcasted_iota(jnp.int32, (1, 128), 1)
    for s in range(seqs):
        keys = k[s]
        logits = lax.dot_general(q[s], keys, (((1,), (1,)), ((), ())), preferred_element_type=F32)
        logits = logits + lax.dot_general(
            qr[s], kr[s], (((0,), (0,)), ((), ())), preferred_element_type=F32)
        logits = logits * (NOPE + rope) ** (-0.5)
        visible = position < lens[s]
        logits = jnp.where(visible, logits, NEGATIVE_PADDING)
        top = jnp.max(logits, axis=1, keepdims=True)
        weights = jnp.where(visible, jnp.exp(logits - top), 0.0)
        total = jnp.sum(weights, axis=1, keepdims=True)
        weighted = jnp.dot(weights.astype(BF16), keys, preferred_element_type=F32)
        both = jnp.where(lane < 64, top, total)
        for p in range(ncol):
            cut = slice(p * hs, (p + 1) * hs)
            att[p, s] = weighted[cut].astype(BF16)
            stat[p, s] = both[cut]
    for d in range(1, ncol):
        for copy in att_copies(d):
            copy.start()

    for d in range(1, nrow):
        x_copy(d, lax.rem(r - d + nrow, nrow)).wait()
    wide = xall[...].astype(F32).reshape(tokens, feats)
    squares = jnp.sum(wide * wide, axis=1, keepdims=True)
    sq[...] = jnp.broadcast_to(squares, (tokens, 128)).reshape(ncol, tb, 128)
    xg[...] = (wide * gain[...].astype(F32)).astype(BF16)

    def sq_copy(d):
        peer = lax.rem(c + d, ncol)
        return remote(sq.at[peer], sq_in.at[d - 1], sq_ss.at[d - 1], sq_rs.at[d - 1], "col", peer)

    for d in range(1, ncol):
        sq_copy(d).start()

    def gu_copy(j, d):
        peer = lax.rem(c + d, ncol)
        return remote(gu.at[j, peer], gu_in.at[j, d - 1], gu_ss.at[j, d - 1], gu_rs.at[j, d - 1],
                      "col", peer)

    def h_copy(j, d, source):
        return remote(hid.at[j, c], hid.at[j, source], h_ss.at[j, d - 1], h_rs.at[j, d - 1],
                      "col", lax.rem(c + d, ncol))

    def project(j):
        copies = weight_copies(j)
        copies[0].wait()
        gate = jnp.dot(xg[...], wg[j], preferred_element_type=F32).astype(BF16)
        for p in range(ncol):
            gu[j, p, 0] = gate[p * tb:(p + 1) * tb]
        copies[1].wait()
        up = jnp.dot(xg[...], wu[j], preferred_element_type=F32).astype(BF16)
        for p in range(ncol):
            gu[j, p, 1] = up[p * tb:(p + 1) * tb]
        for d in range(1, ncol):
            gu_copy(j, d).start()

    def activate(j, norm):
        for d in range(1, ncol):
            gu_copy(j, d).wait_recv()
        gate = gu[j, c, 0].astype(F32)
        up = gu[j, c, 1].astype(F32)
        for d in range(1, ncol):
            gate = gate + gu_in[j, d - 1, 0].astype(F32)
            up = up + gu_in[j, d - 1, 1].astype(F32)
        gate = gate * norm
        hid[j, c] = (gate / (1.0 + jnp.exp(-gate)) * (up * norm)).astype(BF16)
        for d in range(1, ncol):
            h_copy(j, d, c).start()

    project(0)
    for d in range(1, ncol):
        sq_copy(d).wait()
    mean = sq[c]
    for d in range(1, ncol):
        mean = mean + sq_in[d - 1]
    norm = lax.rsqrt(mean[:, :1] / (feats * ncol) + 1e-06)

    @pl.loop(1, chunks)
    def _(j):
        project(j)
        activate(j - 1, norm)

    activate(chunks - 1, norm)

    acc[...] = jnp.zeros_like(acc)

    @pl.loop(0, chunks)
    def _(j):
        weight_copies(j)[2].wait()
        for d in range(1, ncol):
            h_copy(j, d, lax.rem(c - d + ncol, ncol)).wait_recv()
        hidden = hid[j].astype(F32).reshape(tokens, nb).astype(BF16)
        acc[...] += jnp.dot(hidden, wd[j], preferred_element_type=F32)

    dn[...] = acc[...].reshape(nrow, own_rows, feats).astype(BF16)

    def dn_copy(d):
        peer = lax.rem(r + d, nrow)
        return remote(dn.at[peer], dn_in.at[d - 1], dn_ss.at[d - 1], dn_rs.at[d - 1], "row", peer)

    for d in range(1, nrow):
        dn_copy(d).start()

    for d in range(1, ncol):
        for copy in att_copies(d):
            copy.wait()
    for s in range(seqs):
        tops = [stat[c, s, :, 0:1]] + [stat_in[d - 1, s, :, 0:1] for d in range(1, ncol)]
        totals = [stat[c, s, :, 64:65]] + [stat_in[d - 1, s, :, 64:65] for d in range(1, ncol)]
        parts = [att[c, s]] + [att_in[d - 1, s] for d in range(1, ncol)]
        top = functools.reduce(jnp.maximum, tops)
        factors = [jnp.exp(t - top) for t in tops]
        total = sum(f * t for f, t in zip(factors, totals))
        weighted = sum(f * w.astype(F32) for f, w in zip(factors, parts))
        ctx_ref[s] = (weighted / total).astype(BF16)

    own = xall[r].astype(F32)
    summed = acc[pl.ds(pl.multiple_of(r * own_rows, own_rows), own_rows), :]
    for d in range(1, nrow):
        dn_copy(d).wait()
        summed = summed + dn_in[d - 1].astype(F32)
    out_ref[...] = (own + summed).astype(BF16)

    @pl.loop(0, chunks)
    def _(j):
        for d in range(1, ncol):
            gu_copy(j, d).wait_send()
            h_copy(j, d, c).wait_send()


def on_device(nrow, ncol, q, qr, k, kr, lens, x, gain, wg, wu, wd):
    seqs, heads, latent = q.shape
    own_rows, feats = x.shape
    units = wg.shape[1]
    tokens = own_rows * nrow
    tb, hs = tokens // ncol, heads // ncol
    chunks = 1
    for n in (6, 4, 3, 2):
        if units % (256 * n) == 0:
            chunks = n
            break
    nb = units // chunks
    dma = pltpu.SemaphoreType.DMA
    anywhere = pl.BlockSpec(memory_space=pl.ANY)
    vmem = pl.BlockSpec(memory_space=pltpu.VMEM)
    return pl.pallas_call(
        functools.partial(kernel, nrow, ncol, chunks),
        out_shape=(
            jax.ShapeDtypeStruct((seqs, hs, latent), BF16),
            jax.ShapeDtypeStruct((own_rows, feats), BF16),
        ),
        in_specs=[anywhere] * 4 + [pl.BlockSpec(memory_space=pltpu.SMEM)] + [anywhere] * 5,
        out_specs=(vmem, vmem),
        scratch_shapes=[
            pltpu.VMEM(q.shape, BF16),
            pltpu.VMEM(qr.shape, BF16),
            pltpu.VMEM(k.shape, BF16),
            pltpu.VMEM(kr.shape, BF16),
            pltpu.VMEM((1, feats), BF16),
            pltpu.VMEM((nrow, own_rows, feats), BF16),
            pltpu.VMEM((tokens, feats), BF16),
            pltpu.VMEM((chunks, feats, nb), BF16),
            pltpu.VMEM((chunks, feats, nb), BF16),
            pltpu.VMEM((chunks, nb, feats), BF16),
            pltpu.VMEM((ncol, seqs, hs, latent), BF16),
            pltpu.VMEM((ncol, seqs, hs, 128), F32),
            pltpu.VMEM((ncol - 1, seqs, hs, latent), BF16),
            pltpu.VMEM((ncol - 1, seqs, hs, 128), F32),
            pltpu.VMEM((ncol, tb, 128), F32),
            pltpu.VMEM((ncol - 1, tb, 128), F32),
            pltpu.VMEM((chunks, ncol, 2, tb, nb), BF16),
            pltpu.VMEM((chunks, ncol - 1, 2, tb, nb), BF16),
            pltpu.VMEM((chunks, ncol, tb, nb), BF16),
            pltpu.VMEM((tokens, feats), F32),
            pltpu.VMEM((nrow, own_rows, feats), BF16),
            pltpu.VMEM((nrow - 1, own_rows, feats), BF16),
            dma((6,)),
            dma((3, chunks)),
            dma((nrow - 1,)), dma((nrow - 1,)),
            dma((ncol - 1,)), dma((ncol - 1,)),
            dma((ncol - 1,)), dma((ncol - 1,)),
            dma((ncol - 1,)), dma((ncol - 1,)),
            dma((chunks, ncol - 1)), dma((chunks, ncol - 1)),
            dma((chunks, ncol - 1)), dma((chunks, ncol - 1)),
            dma((nrow - 1,)), dma((nrow - 1,)),
        ],
        compiler_params=pltpu.CompilerParams(
            collective_id=0, has_side_effects=True, vmem_limit_bytes=67043328
        ),
    )(q, qr, k, kr, lens, x, gain[None, :], wg, wu, wd)


def solution(mesh):
    return jax.shard_map(
        functools.partial(on_device, mesh.shape["row"], mesh.shape["col"]),
        mesh=mesh,
        in_specs=(
            P(("group", "row"), None, None),
            P(("group", "row"), None, None),
            P(("group", "row"), "col", None),
            P(("group", "row"), None, "col"),
            P(("group", "row")),
            P(("group", "row"), "col"),
            P("col"),
            P("col", "row"),
            P("col", "row"),
            P("row", "col"),
        ),
        out_specs=(P(("group", "row"), "col", None), P(("group", "row"), "col")),
        check_vma=False,
    )
```

time: 116 us -> 54.1 us (0.47)
  Pallas kernels: 0 us -> 49.1 us
  blocking collectives: 38.1 us -> 0 us
  waiting for transfers between devices: 28.8 us -> 0 us
  matrix products: 22.7 us -> 0 us
  between operations: 13.9 us -> 0.64 us
  other arithmetic: 11.3 us -> 0 us
  local copies, waits for them, and re-layouts: 0.12 us -> 4.12 us
    pallas_call x0 -> x1, Pallas kernels: none -> 49.1 us  [on_device(): pl.pallas_call(functools.partial(kernel, nrow, ncol, chunks), out_shape=(...]
    all_gather x4 -> x0, blocking collectives: 29.7 us -> none  [the longest x1 13.7 us: on_device(): shard_rows = lax.all_gather(normed, 'row', axis=0, tiled=True)]
    reduce_scatter x2 -> x0, waiting for transfers between devices: 27 us -> none  [the longest x1 16.8 us: on_device(): lax.psum_scatter(jnp.dot(hidden, w_down, preferred_element_type=jnp.float...]
    dot_general x6 -> x0, matrix products: 22.7 us -> none  [the longest x1 9.63 us: on_device(): jnp.dot(hidden, w_down, preferred_element_type=jnp.float32)]
    psum x1 -> x0, blocking collectives: 8.34 us -> none  [on_device(): square_sums = lax.psum(jnp.sum(rows_wide * rows_wide, axis=1), 'col')]
    convert_element_type x9 -> x0, other arithmetic: 5.8 us -> none  [the longest x1 1.43 us: on_device(): ffn_out = (rows_wide + reduced_total).astype(jnp.bfloat16)]
    add x7 -> x0, other arithmetic: 3.44 us -> none  [the longest x3 3.36 us: join_partials(): earlier[2] * left_factor[:, :, None] + later[2] * right_factor[:, :, None]]
    unnamed x14 -> x2, local copies, waits for them, and re-layouts: 0.04 us -> 2.83 us
  transfers between devices with their start and end apart: 3 -> 0, of which waited for: 3 -> 0; matrix products, arithmetic and copies ran while one was open for 15% -> 0% of each run, Pallas kernels for 0% -> 0%
where the time goes in v1:
time: 54.1 us; the launch traced here: 53.8 us
  Pallas kernels  49.1 us (91%)
  local copies, waits for them, and re-layouts  4.12 us (8%)
  between operations  0.64 us (1%)
    pallas_call x1, Pallas kernels, on_device(): pl.pallas_call(functools.partial(kernel, nrow, ncol, chunks), out_shape=(...  49.1 us
    unnamed x2, local copies, waits for them, and re-layouts  2.83 us
    broadcast_in_dim x1, local copies, waits for them, and re-layouts, on_device(): gain[None, :]  1.29 us

profile of v1, /device:TPU:0, one launch (start us, length us, event | category | flops | bytes accessed | tf_op | source)
XLA Modules:
  0.0 53.8 jit_solution(5680112391846998142)
XLA Ops:
  0.6 1.3 %broadcast_in_dim.3.gain_hbm = bf16[1,1792]{1,0:T(2,128)(2,1)} reshape(bf16[1792]{0:T(1024)(128)(2,1)} %param.16) | data formatting | bytes 7168 | tf_op jit(solution)/shard_map/broadcast_in_dim | solution.py:293
  1.9 49.1 %shard_map.113 = (bf16[2,32,512]{2,1,0:T(8,128)(2,1)}, bf16[8,1792]{1,0:T(8,128)(2,1)}) custom-call(bf16[2,128,512]{2,1,0:T(8,128)(2,1)} %q_hbm.1, bf16[2,64,128]{2,1,0:T(8,128)(2,1)} %qr_hbm.1, bf16[2,256,512]{2,1,0:T(8,128)(2,1)} %k_hbm.1, bf16[2,64,256]{2,1,0:T(8,128)(2,1)} %kr_hbm.1, s32[2]{0:T(128)} %lens.1, bf16[8,1792]{1,0:T(8,128)(2,1)} %x_hbm.1, ...), custom_call_target="tpu_custom_call" | custom-call | tf_op jit(solution)/shard_map/pallas_call | solution.py:249
  51.0 1.5 %copy.14 = bf16[2,32,512]{2,1,0:T(8,128)(2,1)} copy(bf16[2,32,512]{2,1,0:T(8,128)(2,1)} %get-tuple-element.4) | data formatting | bytes 131072
  52.5 1.4 %copy.15 = bf16[8,1792]{1,0:T(8,128)(2,1)} copy(bf16[8,1792]{1,0:T(8,128)(2,1)} %get-tuple-element.5) | data formatting | bytes 57344

commit v2 on v1

--- a/solution.py
+++ b/solution.py
@@ -126,7 +126,7 @@
     wide = xall[...].astype(F32).reshape(tokens, feats)
     squares = jnp.sum(wide * wide, axis=1, keepdims=True)
     sq[...] = jnp.broadcast_to(squares, (tokens, 128)).reshape(ncol, tb, 128)
-    xg[...] = (wide * gain[...].astype(F32)).astype(BF16)
+    xg[...] = (wide * gain[...].astype(F32)[None, :]).astype(BF16)
 
     def sq_copy(d):
         peer = lax.rem(c + d, ncol)
@@ -178,12 +178,20 @@
         mean = mean + sq_in[d - 1]
     norm = lax.rsqrt(mean[:, :1] / (feats * ncol) + 1e-06)
 
-    @pl.loop(1, chunks)
+    lag = min(3, chunks)
+
+    @pl.loop(1, lag)
     def _(j):
         project(j)
-        activate(j - 1, norm)
-
-    activate(chunks - 1, norm)
+
+    @pl.loop(lag, chunks)
+    def _(j):
+        project(j)
+        activate(j - lag, norm)
+
+    @pl.loop(chunks - lag, chunks)
+    def _(j):
+        activate(j, norm)
 
     acc[...] = jnp.zeros_like(acc)
 
@@ -238,7 +246,7 @@
     tokens = own_rows * nrow
     tb, hs = tokens // ncol, heads // ncol
     chunks = 1
-    for n in (6, 4, 3, 2):
+    for n in (3, 4, 6, 2):
         if units % (256 * n) == 0:
             chunks = n
             break
@@ -259,7 +267,7 @@
             pltpu.VMEM(qr.shape, BF16),
             pltpu.VMEM(k.shape, BF16),
             pltpu.VMEM(kr.shape, BF16),
-            pltpu.VMEM((1, feats), BF16),
+            pltpu.VMEM((feats,), BF16),
             pltpu.VMEM((nrow, own_rows, feats), BF16),
             pltpu.VMEM((tokens, feats), BF16),
             pltpu.VMEM((chunks, feats, nb), BF16),
@@ -290,7 +298,7 @@
         compiler_params=pltpu.CompilerParams(
             collective_id=0, has_side_effects=True, vmem_limit_bytes=67043328
         ),
-    )(q, qr, k, kr, lens, x, gain[None, :], wg, wu, wd)
+    )(q, qr, k, kr, lens, x, gain, wg, wu, wd)
 
 
 def solution(mesh):

time: 54.1 us -> 47.4 us (0.88)
  Pallas kernels: 49.1 us -> 43.7 us
  local copies, waits for them, and re-layouts: 4.12 us -> 2.83 us
    pallas_call x1, Pallas kernels: 49.1 us -> 43.7 us  [on_device(): pl.pallas_call(functools.partial(kernel, nrow, ncol, chunks), out_shape=(...]
    broadcast_in_dim x1 -> x0, local copies, waits for them, and re-layouts: 1.29 us -> none  [on_device(): gain[None, :]]
where the time goes in v2:
time: 47.4 us; the launch traced here: 47.2 us
  Pallas kernels  43.7 us (92%)
  local copies, waits for them, and re-layouts  2.83 us (6%)
  between operations  0.64 us (1%)
    pallas_call x1, Pallas kernels, on_device(): pl.pallas_call(functools.partial(kernel, nrow, ncol, chunks), out_shape=(...  43.7 us
    unnamed x2, local copies, waits for them, and re-layouts  2.83 us

profile of v2, /device:TPU:0, one launch (start us, length us, event | category | flops | bytes accessed | tf_op | source)
XLA Modules:
  0.0 47.2 jit_solution(18157592961314102736)
XLA Ops:
  0.6 43.7 %shard_map.113 = (bf16[2,32,512]{2,1,0:T(8,128)(2,1)}, bf16[8,1792]{1,0:T(8,128)(2,1)}) custom-call(bf16[2,128,512]{2,1,0:T(8,128)(2,1)} %q_hbm.1, bf16[2,64,128]{2,1,0:T(8,128)(2,1)} %qr_hbm.1, bf16[2,256,512]{2,1,0:T(8,128)(2,1)} %k_hbm.1, bf16[2,64,256]{2,1,0:T(8,128)(2,1)} %kr_hbm.1, s32[2]{0:T(128)} %lens.1, bf16[8,1792]{1,0:T(8,128)(2,1)} %x_hbm.1, ...), custom_call_target="tpu_custom_call" | custom-call | tf_op jit(solution)/shard_map/pallas_call | solution.py:257
  44.4 1.5 %copy.14 = bf16[2,32,512]{2,1,0:T(8,128)(2,1)} copy(bf16[2,32,512]{2,1,0:T(8,128)(2,1)} %get-tuple-element.4) | data formatting | bytes 131072
  45.8 1.4 %copy.15 = bf16[8,1792]{1,0:T(8,128)(2,1)} copy(bf16[8,1792]{1,0:T(8,128)(2,1)} %get-tuple-element.5) | data formatting | bytes 57344
